TPU v7x, 32 devices: a whole 2x2x4 slice. The times are simulated.
32 devices in a mesh: seq: 8 (over z, x), res: 4 (over y, core).
Axes of the slice: x: 2, y: 2, z: 4, core: 2. Of those that a mesh axis runs over, the one named last changes fastest.
Arguments:
- alignment: bfloat16 [128, 4, 128, 256], P('seq', 'res'), may hold values from -8 to 8
- gain_attn: float32 [256], replicated, may hold values from 0.1 to 1.9
- w_proj: bfloat16 [256, 4, 256], replicated, may hold values from -0.75 to 0.75
- w_out: bfloat16 [256, 256], replicated, may hold values from -0.375 to 0.375
- gain_head: float32 [256], replicated, may hold values from 0.1 to 1.9
- w_head: bfloat16 [256, 23], replicated, may hold values from -1 to 1
- masked: int32 [128, 4, 128], P('res', None, 'seq'), may hold values from 0 to 1
- labels: int32 [128, 4, 128], P('res', None, 'seq'), may hold values from 0 to 22
Outputs:
- updated: bfloat16 [128, 4, 128, 256], P('res', None, 'seq')
- masked_loss: float32 [], replicated
- mask_share: float32 [], replicated
All inputs are finite; a program needn't handle non-finite values.
Results may differ from a plain program's by a relative error of at most 0.011.
Values may be sent and summed in bfloat16 or wider, within the bound.
A program may use at most 192 MiB of HBM per device.

v0:
```python
import jax
import jax.numpy as jnp
from jax import lax
from jax.sharding import PartitionSpec as P

HEADS = 8
HEAD_DIM = 32


def normalize(values, gain):
    mean = jnp.mean(values, axis=-1, keepdims=True)
    centred = values - mean
    spread = jnp.mean(centred * centred, axis=-1, keepdims=True)
    return centred * lax.rsqrt(spread + 1e-05) * gain


def project(flat_rows, gain_attn, w_proj):
    features = flat_rows.shape[1]
    normed = normalize(flat_rows.astype(jnp.float32), gain_attn).astype(jnp.bfloat16)
    return jnp.dot(
        normed, w_proj.reshape(features, 4 * features), preferred_element_type=jnp.float32
    ).astype(jnp.bfloat16)


def column_attention(queries, key_part, value_part):
    inv_root = HEAD_DIM ** (-0.5)
    scores = (
        jnp.einsum("shd,thd->hst", queries, key_part, preferred_element_type=jnp.float32) * inv_root
    )
    probs = jnp.exp(scores)
    totals = jnp.sum(probs, axis=2)
    weighted = jnp.einsum(
        "hst,thd->shd", probs.astype(jnp.bfloat16), value_part, preferred_element_type=jnp.float32
    )
    return (weighted, totals)


def finish(flat_rows, gated, w_out):
    summed = flat_rows.astype(jnp.float32) + jnp.dot(
        gated, w_out, preferred_element_type=jnp.float32
    )
    return summed.astype(jnp.bfloat16)


def on_device(alignment, gain_attn, w_proj, w_out, gain_head, w_head, masked, labels):
    weights = masked.reshape(-1).astype(jnp.float32)
    local_count = jnp.sum(weights)
    local_rows, single_block, segment, features = alignment.shape
    seq_devices = lax.axis_size("seq")
    split_view = alignment.reshape(local_rows, seq_devices, segment // seq_devices, features)
    column_block = lax.all_to_all(split_view, "seq", split_axis=1, concat_axis=0, tiled=True)
    seq_total, single, col_count, features = column_block.shape
    by_column = jnp.transpose(column_block.reshape(seq_total, col_count, features), (1, 0, 2))
    flat_rows = by_column.reshape(col_count * seq_total, features)
    projected = project(flat_rows, gain_attn, w_proj).reshape(
        col_count, seq_total, 4, HEADS, HEAD_DIM
    )

    def per_column(picked):
        weighted, totals = column_attention(picked[:, 0], picked[:, 1], picked[:, 2])
        attended = weighted / totals.T[:, :, None]
        gated_col = attended * jax.nn.sigmoid(picked[:, 3].astype(jnp.float32))
        return gated_col.reshape(seq_total, features).astype(jnp.bfloat16)

    gated = lax.map(per_column, projected).reshape(col_count * seq_total, features)
    result = finish(flat_rows, gated, w_out).reshape(col_count, seq_total, features)
    result = jnp.transpose(result, (1, 0, 2)).reshape(seq_total, single, col_count, features)
    updated = lax.all_to_all(result, "res", split_axis=0, concat_axis=1, tiled=True)
    features = updated.shape[3]
    flat_out = updated.reshape(-1, features)
    head_in = normalize(flat_out.astype(jnp.float32), gain_head).astype(jnp.bfloat16)
    logits = jnp.einsum("rc,ck->kr", head_in, w_head, preferred_element_type=jnp.float32)
    log_total = jnp.log(jnp.sum(jnp.exp(logits), axis=0))
    classes = jnp.arange(logits.shape[0], dtype=jnp.int32)[:, None]
    picked = jnp.sum(jnp.where(classes == labels.reshape(1, -1), logits, 0.0), axis=0)
    errors = log_total - picked
    local_loss = jnp.sum(errors * weights)
    loss_sum, mask_count = lax.psum((local_loss, local_count), ("seq", "res"))
    entries = flat_out.shape[0] * lax.axis_size("seq") * lax.axis_size("res")
    masked_loss = loss_sum / (1.0 + mask_count)
    mask_share = mask_count / entries
    return (updated, masked_loss, mask_share)


def solution(mesh):
    in_specs = (
        P("seq", "res", None, None),
        P(),
        P(),
        P(),
        P(),
        P(),
        P("res", None, "seq"),
        P("res", None, "seq"),
    )
    out_specs = (P("res", None, "seq", None), P(), P())
    return jax.shard_map(
        on_device, mesh=mesh, in_specs=in_specs, out_specs=out_specs, check_vma=False
    )
```

profile of v0, /device:TPU:12, one launch (start us, length us, event | category | flops | bytes accessed | tf_op | source)
XLA Modules:
  0.0 152.1 jit_solution(10787070603162363327)
XLA Ops:
  0.7 2.4 %copy.61 = bf16[16,8,16,256]{3,2,0,1:T(8,128)(2,1)} copy(bf16[16,8,16,256]{3,2,1,0:T(8,128)(2,1)} %bitcast.113) | data formatting | bytes 2097152 | tf_op jit(solution)/shard_map/reshape | solution.py:50
  3.0 6.3 %all-to-all-start = ((bf16[16,8,16,256]{3,2,0,1:T(8,128)(2,1)}), bf16[16,8,16,256]{3,2,0,1:T(8,128)(2,1)S(1)}, u32[]{:S(2)}, u32[]{:S(2)}) async-start(bf16[16,8,16,256]{3,2,0,1:T(8,128)(2,1)} %copy.61), calls=%async_computation | async-start | bytes 2097152 | tf_op jit(solution)/shard_map/all_to_all | solution.py:51
  9.4 23.3 %all-to-all-done = bf16[16,8,16,256]{3,2,0,1:T(8,128)(2,1)S(1)} async-done(((bf16[16,8,16,256]{3,2,0,1:T(8,128)(2,1)}), bf16[16,8,16,256]{3,2,0,1:T(8,128)(2,1)S(1)}, u32[]{:S(2)}, u32[]{:S(2)}) %all-to-all-start) | async-done | bytes 1048608 | tf_op jit(solution)/shard_map/all_to_all | solution.py:51
  32.9 1.2 bitcast_reduce_fusion
  34.1 1.2 copy.62
  35.3 1.6 %multiply_reduce_fusion.1 = f32[16,128]{1,0:T(8,128)S(1)} fusion(f32[16,128]{1,0:T(8,128)S(1)} %broadcast_multiply_fusion.1, f32[128,16,256]{2,1,0:T(8,128)S(1)} %bitcast.100), kind=kLoop, calls=%fused_computation.24 | loop fusion | flops 1570816 | bytes 2113536 | tf_op jit(solution)/shard_map/reduce_sum | solution.py:13
  37.0 1.4 multiply_convert_fusion
  38.3 3.2 %convolution_convert_fusion = bf16[2048,1024]{1,0:T(8,128)(2,1)} fusion(bf16[2048,256]{1,0:T(8,128)(2,1)S(1)} %bitcast.109, bf16[256,1024]{1,0:T(8,128)(2,1)S(1)} %bitcast.111), kind=kOutput, calls=%fused_computation.12 | convolution fusion | flops 1075838976 | bytes 5767168 | tf_op jit(solution)/shard_map/dot_general | solution.py:20
  41.5 6.5 %copy.63 = bf16[2048,1024]{0,1:T(8,128)(2,1)} copy(bf16[2048,1024]{1,0:T(8,128)(2,1)} %convolution_convert_fusion) | data formatting | bytes 8388608 | tf_op jit(solution)/shard_map/convert_element_type | solution.py:22
  48.0 3.6 %copy.80 = bf16[128,8,16,128]{3,2,1,0:T(8,128)(2,1)S(1)} copy(bf16[128,8,16,128]{3,1,2,0:T(8,128)(2,1)} %bitcast.106) | data formatting | bytes 8388608
  51.6 3.0 %copy.64 = bf16[16,128,4,8,32]{1,4,3,2,0:T(8,128)(2,1)} copy(bf16[16,128,4,8,32]{1,0,4,3,2:T(8,128)(2,1)S(1)} %bitcast.107) | data formatting | bytes 8388608 | tf_op jit(solution)/shard_map/while | solution.py:65
  54.7 26.1 %while.10 = (s32[]{:T(128)}, bf16[16,128,256]{2,1,0:T(8,128)(2,1)S(1)}, bf16[16,128,4,8,32]{1,4,3,2,0:T(8,128)(2,1)}, s32[]{:T(128)}) while((s32[]{:T(128)}, bf16[16,128,256]{2,1,0:T(8,128)(2,1)S(1)}, bf16[16,128,4,8,32]{1,4,3,2,0:T(8,128)(2,1)}, s32[]{:T(128)}) %tuple.42), condition=%wide.region_4.0_spmd, body=%wide.region_2.4_spmd.sunk | while | flops 17398784 | bytes 1646653 | solution.py:65
  56.3 1.0 dynamic-slice_bitcast_fusion.2
  57.9 1.0 dynamic-slice_bitcast_fusion.2
  59.6 1.0 dynamic-slice_bitcast_fusion.2
  61.2 1.0 dynamic-slice_bitcast_fusion.2
  62.8 1.0 dynamic-slice_bitcast_fusion.2
  64.5 1.0 dynamic-slice_bitcast_fusion.2
  66.1 1.0 dynamic-slice_bitcast_fusion.2
  67.7 1.0 dynamic-slice_bitcast_fusion.2
  69.4 1.0 dynamic-slice_bitcast_fusion.2
  71.0 1.0 dynamic-slice_bitcast_fusion.2
  72.6 1.0 dynamic-slice_bitcast_fusion.2
  74.3 1.0 dynamic-slice_bitcast_fusion.2
  75.9 1.0 dynamic-slice_bitcast_fusion.2
  77.5 1.0 dynamic-slice_bitcast_fusion.2
  81.3 1.6 %copy.85 = bf16[16,128,256]{2,0,1:T(8,128)(2,1)} copy(bf16[16,128,256]{2,1,0:T(8,128)(2,1)S(1)} %bitcast.110) | data formatting | bytes 2097152 | tf_op jit(solution)/shard_map/reshape | solution.py:66
  82.8 4.0 %all-to-all-start.1 = ((bf16[128,1,16,256]{3,2,1,0:T(8,128)(2,1)}), bf16[128,1,16,256]{3,2,1,0:T(8,128)(2,1)S(1)}, u32[]{:S(2)}, u32[]{:S(2)}) async-start(bf16[128,1,16,256]{3,2,1,0:T(8,128)(2,1)} %bitcast.79), calls=%async_computation.1 | async-start | bytes 2097152 | tf_op jit(solution)/shard_map/all_to_all | solution.py:68
  87.1 12.5 %all-to-all-done.1 = bf16[128,1,16,256]{3,2,1,0:T(8,128)(2,1)S(1)} async-done(((bf16[128,1,16,256]{3,2,1,0:T(8,128)(2,1)}), bf16[128,1,16,256]{3,2,1,0:T(8,128)(2,1)S(1)}, u32[]{:S(2)}, u32[]{:S(2)}) %all-to-all-start.1) | async-done | bytes 1048608 | tf_op jit(solution)/shard_map/all_to_all | solution.py:68
  102.5 1.1 exponential_reduce_fusion
  104.4 42.4 %all-reduce = (f32[]{:T(128)}, f32[]{:T(128)}) all-reduce(f32[]{:T(128)} %get-tuple-element.57, f32[]{:T(128)} %get-tuple-element.56), channel_id=1, replica_groups=mesh['seq'=8,'res'=4] {'seq','res'}, use_global_device_ids=true, to_apply=%region_10.11 | all-reduce | flops 2 | bytes 16 | tf_op jit(solution)/shard_map/psum | solution.py:78
  148.1 1.1 copy.75
  (105 shorter events, 16.6 us)
Async XLA Ops:
  0.6 80.2 %copy-start = (bf16[256,256]{1,0:T(8,128)(2,1)S(1)}, bf16[256,256]{1,0:T(8,128)(2,1)}, u32[]{:S(2)}) copy-start(bf16[256,256]{1,0:T(8,128)(2,1)} %param.13) | copy-start | bytes 393220
  0.6 8.6 %copy-start.2 = (bf16[256,4,256]{2,1,0:T(4,128)(2,1)S(1)}, bf16[256,4,256]{2,1,0:T(4,128)(2,1)}, u32[]{:S(2)}) copy-start(bf16[256,4,256]{2,1,0:T(4,128)(2,1)} %param.12) | copy-start | bytes 1572868
  3.0 29.6 %all-to-all-start = ((bf16[16,8,16,256]{3,2,0,1:T(8,128)(2,1)}), bf16[16,8,16,256]{3,2,0,1:T(8,128)(2,1)S(1)}, u32[]{:S(2)}, u32[]{:S(2)}) async-start(bf16[16,8,16,256]{3,2,0,1:T(8,128)(2,1)} %copy.61), calls=%async_computation | async-start | bytes 2097152 | tf_op jit(solution)/shard_map/all_to_all | solution.py:51
  35.3 1.7 %copy-start.5 = (f32[256]{0:T(256)S(1)}, f32[256]{0:T(256)}, u32[]{:S(2)}) copy-start(f32[256]{0:T(256)} %param.11) | copy-start | bytes 3076
  51.6 3.0 %copy-start.1 = (bf16[16,128,256]{2,1,0:T(8,128)(2,1)S(1)}, bf16[16,128,256]{2,1,0:T(8,128)(2,1)}, u32[]{:S(2)}) copy-start(bf16[16,128,256]{2,1,0:T(8,128)(2,1)} %custom-call) | copy-start | bytes 3145732
  81.3 5.6 %copy-start.3 = (s32[32,4,16]{0,2,1:T(8,128)S(1)}, s32[32,4,16]{0,2,1:T(8,128)}, u32[]{:S(2)}) copy-start(s32[32,4,16]{0,2,1:T(8,128)} %param.17) | copy-start | bytes 24580
  81.3 5.7 %copy-start.4 = (s32[32,4,16]{0,2,1:T(8,128)S(1)}, s32[32,4,16]{0,2,1:T(8,128)}, u32[]{:S(2)}) copy-start(s32[32,4,16]{0,2,1:T(8,128)} %param.16) | copy-start | bytes 24580
  82.8 16.8 %all-to-all-start.1 = ((bf16[128,1,16,256]{3,2,1,0:T(8,128)(2,1)}), bf16[128,1,16,256]{3,2,1,0:T(8,128)(2,1)S(1)}, u32[]{:S(2)}, u32[]{:S(2)}) async-start(bf16[128,1,16,256]{3,2,1,0:T(8,128)(2,1)} %bitcast.79), calls=%async_computation.1 | async-start | bytes 2097152 | tf_op jit(solution)/shard_map/all_to_all | solution.py:68
  100.2 1.4 copy-start.6
where the time goes:
time: 153 us; the launch traced here: 152 us
  blocking collectives  42.4 us (28%)
  local copies, waits for them, and re-layouts  38.2 us (25%)
  waiting for transfers between devices  35.8 us (23%)
  matrix products  12.7 us (8%)
  starting transfers between devices  10.2 us (7%)
  other arithmetic  7 us (5%)
  between operations  5.09 us (3%)
    psum x1, blocking collectives, on_device(): loss_sum, mask_count = lax.psum((local_loss, local_count), ('seq', 'res'))  42.4 us
    all_to_all x1, waiting for transfers between devices, on_device(): lax.all_to_all(split_view, 'seq', split_axis=1, concat_axis=0, tiled=True)  23.3 us
    squeeze x16, local copies, waits for them, and re-layouts, on_device(): lax.map(per_column, projected).reshape(col_count * seq_total, features)  15.5 us
    all_to_all x1, waiting for transfers between devices, on_device(): lax.all_to_all(result, 'res', split_axis=0, concat_axis=1, tiled=True)  12.5 us
    convert_element_type x1, local copies, waits for them, and re-layouts, project(): return jnp.dot(normed, w_proj.reshape(features, 4 * features), preferred_...  6.52 us
    all_to_all x1, starting transfers between devices, on_device(): lax.all_to_all(split_view, 'seq', split_axis=1, concat_axis=0, tiled=True)  6.25 us
    dot_general x16, matrix products, column_attention(): jnp.einsum('shd,thd->hst', queries, key_part, preferred_element_type=jnp....  5.03 us
    unnamed x19, local copies, waits for them, and re-layouts  4.99 us
  transfers between devices with their start and end apart: 2, of which 2 were waited for; matrix products, arithmetic and copies ran while one was open for 0% of the time, Pallas kernels for 0%

commit v1 on v0

--- a/solution.py
+++ b/solution.py
@@ -48,7 +48,17 @@
     local_rows, single_block, segment, features = alignment.shape
     seq_devices = lax.axis_size("seq")
     split_view = alignment.reshape(local_rows, seq_devices, segment // seq_devices, features)
-    column_block = lax.all_to_all(split_view, "seq", split_axis=1, concat_axis=0, tiled=True)
+    far_arr, vec_out = (lax.axis_size("seq"), lax.axis_index("seq"))
+    h_now = split_view.shape[1] // far_arr
+    y_new = jnp.roll(split_view, -vec_out * h_now, 1)
+    made = [lax.slice_in_dim(y_new, 0, h_now, axis=1)]
+    for j in range(1, far_arr):
+        w1 = lax.slice_in_dim(y_new, j * h_now, (j + 1) * h_now, axis=1)
+        made.append(
+            lax.ppermute(w1, "seq", [(dev_i, (dev_i + j) % far_arr) for dev_i in range(far_arr)])
+        )
+    left_arr = jnp.concatenate(made[::-1], 0)
+    column_block = jnp.roll(left_arr, (vec_out + 1) * made[0].shape[0], 0)
     seq_total, single, col_count, features = column_block.shape
     by_column = jnp.transpose(column_block.reshape(seq_total, col_count, features), (1, 0, 2))
     flat_rows = by_column.reshape(col_count * seq_total, features)

time: 153 us -> 148 us (0.967)
  waiting for transfers between devices: 35.8 us -> 29 us
  starting transfers between devices: 10.2 us -> 13.9 us
  other arithmetic: 7 us -> 4.89 us
    all_to_all x1 -> x0, waiting for transfers between devices: 23.3 us -> none  [on_device(): lax.all_to_all(split_view, 'seq', split_axis=1, concat_axis=0, tiled=True)]
    ppermute x0 -> x7, waiting for transfers between devices: none -> 17.1 us  [on_device(): lax.ppermute(w1, 'seq', [(dev_i, (dev_i + j) % far_arr) for dev_i in rang...]
    ppermute x0 -> x7, starting transfers between devices: none -> 9.87 us  [on_device(): lax.ppermute(w1, 'seq', [(dev_i, (dev_i + j) % far_arr) for dev_i in rang...]
    all_to_all x1 -> x0, starting transfers between devices: 6.25 us -> none  [on_device(): lax.all_to_all(split_view, 'seq', split_axis=1, concat_axis=0, tiled=True)]
    unnamed x19 -> x38, local copies, waits for them, and re-layouts: 4.99 us -> 5.78 us
  transfers between devices with their start and end apart: 2 -> 8, of which waited for: 2 -> 6; matrix products, arithmetic and copies ran while one was open for 0% -> 1% of each run, Pallas kernels for 0% -> 0%
where the time goes in v1:
time: 148 us; the launch traced here: 146 us
  blocking collectives  41.9 us (28%)
  local copies, waits for them, and re-layouts  38.1 us (26%)
  waiting for transfers between devices  29 us (20%)
  starting transfers between devices  13.9 us (9%)
  matrix products  12 us (8%)
  between operations  5.29 us (4%)
  other arithmetic  4.89 us (3%)
    psum x1, blocking collectives, on_device(): loss_sum, mask_count = lax.psum((local_loss, local_count), ('seq', 'res'))  41.9 us
    ppermute x7, waiting for transfers between devices, on_device(): lax.ppermute(w1, 'seq', [(dev_i, (dev_i + j) % far_arr) for dev_i in rang...  17.1 us
    squeeze x16, local copies, waits for them, and re-layouts, on_device(): lax.map(per_column, projected).reshape(col_count * seq_total, features)  15.5 us
    all_to_all x1, waiting for transfers between devices, on_device(): lax.all_to_all(result, 'res', split_axis=0, concat_axis=1, tiled=True)  11.9 us
    ppermute x7, starting transfers between devices, on_device(): lax.ppermute(w1, 'seq', [(dev_i, (dev_i + j) % far_arr) for dev_i in rang...  9.87 us
    convert_element_type x1, local copies, waits for them, and re-layouts, project(): return jnp.dot(normed, w_proj.reshape(features, 4 * features), preferred_...  6.52 us
    unnamed x38, local copies, waits for them, and re-layouts  5.78 us
    dot_general x16, matrix products, column_attention(): jnp.einsum('shd,thd->hst', queries, key_part, preferred_element_type=jnp....  5.03 us
  transfers between devices with their start and end apart: 8, of which 6 were waited for; matrix products, arithmetic and copies ran while one was open for 1% of the time, Pallas kernels for 0%

profile of v1, /device:TPU:12, one launch (start us, length us, event | category | flops | bytes accessed | tf_op | source)
XLA Modules:
  0.0 145.7 jit_solution(7844516990078141470)
XLA Ops:
  0.7 1.8 %copy.52 = bf16[16,8,16,256]{3,0,2,1:T(8,128)(2,1)S(1)} copy(bf16[16,8,16,256]{3,2,1,0:T(8,128)(2,1)} %bitcast.109) | data formatting | bytes 2097152 | tf_op jit(solution)/shard_map/reshape | solution.py:50
  3.7 1.4 collective-permute-start
  5.1 3.6 %collective-permute-start.1 = (bf16[16,1,16,256]{3,0,2,1:T(8,128)(2,1)S(1)}, bf16[16,1,16,256]{3,0,2,1:T(8,128)(2,1)S(1)}, u32[]{:S(2)}, u32[]{:S(2)}) collective-permute-start(bf16[16,1,16,256]{3,0,2,1:T(8,128)(2,1)S(1)} %get-tuple-element.67), channel_id=1, source_target_pairs={{0,24},{4,28},{8,0},{12,4},{16,8},{20,12},{24,16},{28,20},{1,25},{... | collective-permute-start | bytes 393224 | tf_op jit(solution)/shard_map/ppermute | solution.py:58
  8.7 3.3 %collective-permute-start.4 = (bf16[16,1,16,256]{3,0,2,1:T(8,128)(2,1)S(1)}, bf16[16,1,16,256]{3,0,2,1:T(8,128)(2,1)S(1)}, u32[]{:S(2)}, u32[]{:S(2)}) collective-permute-start(bf16[16,1,16,256]{3,0,2,1:T(8,128)(2,1)S(1)} %get-tuple-element.64), channel_id=1, source_target_pairs={{0,12},{4,16},{8,20},{12,24},{16,28},{20,0},{24,4},{28,8},{1,13},{... | collective-permute-start | bytes 393224 | tf_op jit(solution)/shard_map/ppermute | solution.py:58
  12.1 1.6 %collective-permute-start.5 = (bf16[16,1,16,256]{3,0,2,1:T(8,128)(2,1)S(1)}, bf16[16,1,16,256]{3,0,2,1:T(8,128)(2,1)S(1)}, u32[]{:S(2)}, u32[]{:S(2)}) collective-permute-start(bf16[16,1,16,256]{3,0,2,1:T(8,128)(2,1)S(1)} %get-tuple-element.63), channel_id=1, source_target_pairs={{0,8},{4,12},{8,16},{12,20},{16,24},{20,28},{24,0},{28,4},{1,9},{5... | collective-permute-start | bytes 393224 | tf_op jit(solution)/shard_map/ppermute | solution.py:58
  13.7 11.3 %collective-permute-done.1 = bf16[16,1,16,256]{3,0,2,1:T(8,128)(2,1)S(1)} collective-permute-done((bf16[16,1,16,256]{3,0,2,1:T(8,128)(2,1)S(1)}, bf16[16,1,16,256]{3,0,2,1:T(8,128)(2,1)S(1)}, u32[]{:S(2)}, u32[]{:S(2)}) %collective-permute-start.1) | collective-permute-done | bytes 131104 | tf_op jit(solution)/shard_map/ppermute | solution.py:58
  25.1 2.0 %collective-permute-done.2 = bf16[16,1,16,256]{3,0,2,1:T(8,128)(2,1)S(1)} collective-permute-done((bf16[16,1,16,256]{3,0,2,1:T(8,128)(2,1)}, bf16[16,1,16,256]{3,0,2,1:T(8,128)(2,1)S(1)}, u32[]{:S(2)}, u32[]{:S(2)}) %collective-permute-start.2) | collective-permute-done | bytes 131104 | tf_op jit(solution)/shard_map/ppermute | solution.py:58
  27.9 2.7 %collective-permute-done.5 = bf16[16,1,16,256]{3,0,2,1:T(8,128)(2,1)S(1)} collective-permute-done((bf16[16,1,16,256]{3,0,2,1:T(8,128)(2,1)S(1)}, bf16[16,1,16,256]{3,0,2,1:T(8,128)(2,1)S(1)}, u32[]{:S(2)}, u32[]{:S(2)}) %collective-permute-start.5) | collective-permute-done | bytes 131104 | tf_op jit(solution)/shard_map/ppermute | solution.py:58
  33.1 3.2 %convolution_convert_fusion = bf16[2048,1024]{1,0:T(8,128)(2,1)} fusion(bf16[2048,256]{1,0:T(8,128)(2,1)S(1)} %bitcast.105, bf16[256,1024]{1,0:T(8,128)(2,1)S(1)} %bitcast.107), kind=kOutput, calls=%fused_computation.12 | convolution fusion | flops 1075838976 | bytes 5767168 | tf_op jit(solution)/shard_map/dot_general | solution.py:20
  36.3 6.5 %copy.54 = bf16[2048,1024]{0,1:T(8,128)(2,1)} copy(bf16[2048,1024]{1,0:T(8,128)(2,1)} %convolution_convert_fusion) | data formatting | bytes 8388608 | tf_op jit(solution)/shard_map/convert_element_type | solution.py:22
  42.8 3.6 %copy.71 = bf16[128,8,16,128]{3,2,1,0:T(8,128)(2,1)S(1)} copy(bf16[128,8,16,128]{3,1,2,0:T(8,128)(2,1)} %bitcast.102) | data formatting | bytes 8388608
  46.4 3.0 %copy.55 = bf16[16,128,4,8,32]{1,4,3,2,0:T(8,128)(2,1)} copy(bf16[16,128,4,8,32]{1,0,4,3,2:T(8,128)(2,1)S(1)} %bitcast.103) | data formatting | bytes 8388608 | tf_op jit(solution)/shard_map/while | solution.py:75
  49.4 26.1 %while.10 = (s32[]{:T(128)}, bf16[16,128,256]{2,1,0:T(8,128)(2,1)S(1)}, bf16[16,128,4,8,32]{1,4,3,2,0:T(8,128)(2,1)}, s32[]{:T(128)}) while((s32[]{:T(128)}, bf16[16,128,256]{2,1,0:T(8,128)(2,1)S(1)}, bf16[16,128,4,8,32]{1,4,3,2,0:T(8,128)(2,1)}, s32[]{:T(128)}) %tuple.46), condition=%wide.region_4.5_spmd, body=%wide.region_2.4_spmd.sunk | while | flops 17398784 | bytes 1646653 | solution.py:75
  51.1 1.0 dynamic-slice_bitcast_fusion.2
  52.7 1.0 dynamic-slice_bitcast_fusion.2
  54.3 1.0 dynamic-slice_bitcast_fusion.2
  56.0 1.0 dynamic-slice_bitcast_fusion.2
  57.6 1.0 dynamic-slice_bitcast_fusion.2
  59.2 1.0 dynamic-slice_bitcast_fusion.2
  60.9 1.0 dynamic-slice_bitcast_fusion.2
  62.5 1.0 dynamic-slice_bitcast_fusion.2
  64.1 1.0 dynamic-slice_bitcast_fusion.2
  65.8 1.0 dynamic-slice_bitcast_fusion.2
  67.4 1.0 dynamic-slice_bitcast_fusion.2
  69.1 1.0 dynamic-slice_bitcast_fusion.2
  70.7 1.0 dynamic-slice_bitcast_fusion.2
  74.0 1.0 dynamic-slice_bitcast_fusion.2
  76.1 1.6 %copy.73 = bf16[16,128,256]{2,0,1:T(8,128)(2,1)} copy(bf16[16,128,256]{2,1,0:T(8,128)(2,1)S(1)} %bitcast.106) | data formatting | bytes 2097152 | tf_op jit(solution)/shard_map/reshape | solution.py:76
  77.6 4.0 %all-to-all-start = ((bf16[128,1,16,256]{3,2,1,0:T(8,128)(2,1)}), bf16[128,1,16,256]{3,2,1,0:T(8,128)(2,1)S(1)}, u32[]{:S(2)}, u32[]{:S(2)}) async-start(bf16[128,1,16,256]{3,2,1,0:T(8,128)(2,1)} %bitcast.79), calls=%async_computation | async-start | bytes 2097152 | tf_op jit(solution)/shard_map/all_to_all | solution.py:78
  82.5 11.9 %all-to-all-done = bf16[128,1,16,256]{3,2,1,0:T(8,128)(2,1)S(1)} async-done(((bf16[128,1,16,256]{3,2,1,0:T(8,128)(2,1)}), bf16[128,1,16,256]{3,2,1,0:T(8,128)(2,1)S(1)}, u32[]{:S(2)}, u32[]{:S(2)}) %all-to-all-start) | async-done | bytes 1048608 | tf_op jit(solution)/shard_map/all_to_all | solution.py:78
  98.5 41.9 %all-reduce = (f32[]{:T(128)}, f32[]{:T(128)}) all-reduce(f32[]{:T(128)} %get-tuple-element.51, f32[]{:T(128)} %get-tuple-element.50), channel_id=1, replica_groups=mesh['seq'=8,'res'=4] {'seq','res'}, use_global_device_ids=true, to_apply=%region_10.11 | all-reduce | flops 2 | bytes 16 | tf_op jit(solution)/shard_map/psum | solution.py:88
  141.7 1.1 copy.66
  (138 shorter events, 21.6 us)
Async XLA Ops:
  0.6 75.0 %copy-start = (bf16[256,256]{1,0:T(8,128)(2,1)S(1)}, bf16[256,256]{1,0:T(8,128)(2,1)}, u32[]{:S(2)}) copy-start(bf16[256,256]{1,0:T(8,128)(2,1)} %param.13) | copy-start | bytes 393220
  2.5 9.4 %copy-start.2 = (bf16[256,4,256]{2,1,0:T(4,128)(2,1)S(1)}, bf16[256,4,256]{2,1,0:T(4,128)(2,1)}, u32[]{:S(2)}) copy-start(bf16[256,4,256]{2,1,0:T(4,128)(2,1)} %param.12) | copy-start | bytes 1572868
  3.7 8.4 %collective-permute-start = (bf16[16,1,16,256]{3,0,2,1:T(8,128)(2,1)S(1)}, bf16[16,1,16,256]{3,0,2,1:T(8,128)(2,1)S(1)}, u32[]{:S(2)}, u32[]{:S(2)}) collective-permute-start(bf16[16,1,16,256]{3,0,2,1:T(8,128)(2,1)S(1)} %get-tuple-element.68), channel_id=1, source_target_pairs={{0,28},{4,0},{8,4},{12,8},{16,12},{20,16},{24,20},{28,24},{1,29},{... | collective-permute-start | bytes 393224 | tf_op jit(solution)/shard_map/ppermute | solution.py:58
  5.1 20.0 %collective-permute-start.1 = (bf16[16,1,16,256]{3,0,2,1:T(8,128)(2,1)S(1)}, bf16[16,1,16,256]{3,0,2,1:T(8,128)(2,1)S(1)}, u32[]{:S(2)}, u32[]{:S(2)}) collective-permute-start(bf16[16,1,16,256]{3,0,2,1:T(8,128)(2,1)S(1)} %get-tuple-element.67), channel_id=1, source_target_pairs={{0,24},{4,28},{8,0},{12,4},{16,8},{20,12},{24,16},{28,20},{1,25},{... | collective-permute-start | bytes 393224 | tf_op jit(solution)/shard_map/ppermute | solution.py:58
  8.7 18.4 %collective-permute-start.2 = (bf16[16,1,16,256]{3,0,2,1:T(8,128)(2,1)}, bf16[16,1,16,256]{3,0,2,1:T(8,128)(2,1)S(1)}, u32[]{:S(2)}, u32[]{:S(2)}) collective-permute-start(bf16[16,1,16,256]{3,0,2,1:T(8,128)(2,1)} %get-tuple-element.66), channel_id=1, source_target_pairs={{0,20},{4,24},{8,28},{12,0},{16,4},{20,8},{24,12},{28,16},{1,21},{... | collective-permute-start | bytes 393224 | tf_op jit(solution)/shard_map/ppermute | solution.py:58
  8.7 18.4 %collective-permute-start.3 = (bf16[16,1,16,256]{3,0,2,1:T(8,128)(2,1)}, bf16[16,1,16,256]{3,0,2,1:T(8,128)(2,1)S(1)}, u32[]{:S(2)}, u32[]{:S(2)}) collective-permute-start(bf16[16,1,16,256]{3,0,2,1:T(8,128)(2,1)} %get-tuple-element.65), channel_id=1, source_target_pairs={{0,16},{4,20},{8,24},{12,28},{16,0},{20,4},{24,8},{28,12},{1,17},{... | collective-permute-start | bytes 393224 | tf_op jit(solution)/shard_map/ppermute | solution.py:58
  8.7 19.2 %collective-permute-start.4 = (bf16[16,1,16,256]{3,0,2,1:T(8,128)(2,1)S(1)}, bf16[16,1,16,256]{3,0,2,1:T(8,128)(2,1)S(1)}, u32[]{:S(2)}, u32[]{:S(2)}) collective-permute-start(bf16[16,1,16,256]{3,0,2,1:T(8,128)(2,1)S(1)} %get-tuple-element.64), channel_id=1, source_target_pairs={{0,12},{4,16},{8,20},{12,24},{16,28},{20,0},{24,4},{28,8},{1,13},{... | collective-permute-start | bytes 393224 | tf_op jit(solution)/shard_map/ppermute | solution.py:58
  12.1 18.5 %collective-permute-start.5 = (bf16[16,1,16,256]{3,0,2,1:T(8,128)(2,1)S(1)}, bf16[16,1,16,256]{3,0,2,1:T(8,128)(2,1)S(1)}, u32[]{:S(2)}, u32[]{:S(2)}) collective-permute-start(bf16[16,1,16,256]{3,0,2,1:T(8,128)(2,1)S(1)} %get-tuple-element.63), channel_id=1, source_target_pairs={{0,8},{4,12},{8,16},{12,20},{16,24},{20,28},{24,0},{28,4},{1,9},{5... | collective-permute-start | bytes 393224 | tf_op jit(solution)/shard_map/ppermute | solution.py:58
  25.0 5.9 %collective-permute-start.6 = (bf16[16,1,16,256]{3,0,2,1:T(8,128)(2,1)S(1)}, bf16[16,1,16,256]{3,0,2,1:T(8,128)(2,1)S(1)}, u32[]{:S(2)}, u32[]{:S(2)}) collective-permute-start(bf16[16,1,16,256]{3,0,2,1:T(8,128)(2,1)S(1)} %get-tuple-element.62), channel_id=1, source_target_pairs={{0,4},{4,8},{8,12},{12,16},{16,20},{20,24},{24,28},{28,0},{1,5},{5... | collective-permute-start | bytes 393224 | tf_op jit(solution)/shard_map/ppermute | solution.py:58
  31.5 0.9 copy-start.7
  46.4 3.0 %copy-start.1 = (bf16[16,128,256]{2,1,0:T(8,128)(2,1)S(1)}, bf16[16,128,256]{2,1,0:T(8,128)(2,1)}, u32[]{:S(2)}) copy-start(bf16[16,128,256]{2,1,0:T(8,128)(2,1)} %custom-call.1) | copy-start | bytes 3145732
  76.0 5.6 %copy-start.4 = (s32[32,4,16]{0,2,1:T(8,128)S(1)}, s32[32,4,16]{0,2,1:T(8,128)}, u32[]{:S(2)}) copy-start(s32[32,4,16]{0,2,1:T(8,128)} %param.17) | copy-start | bytes 24580
  76.0 5.8 %copy-start.5 = (s32[32,4,16]{0,2,1:T(8,128)S(1)}, s32[32,4,16]{0,2,1:T(8,128)}, u32[]{:S(2)}) copy-start(s32[32,4,16]{0,2,1:T(8,128)} %param.16) | copy-start | bytes 24580
  77.6 16.8 %all-to-all-start = ((bf16[128,1,16,256]{3,2,1,0:T(8,128)(2,1)}), bf16[128,1,16,256]{3,2,1,0:T(8,128)(2,1)S(1)}, u32[]{:S(2)}, u32[]{:S(2)}) async-start(bf16[128,1,16,256]{3,2,1,0:T(8,128)(2,1)} %bitcast.79), calls=%async_computation | async-start | bytes 2097152 | tf_op jit(solution)/shard_map/all_to_all | solution.py:78
  94.8 1.6 %copy-start.8 = (f32[256]{0:T(256)S(1)}, f32[256]{0:T(256)}, u32[]{:S(2)}) copy-start(f32[256]{0:T(256)} %param.14) | copy-start | bytes 3076
  95.3 2.0 %copy-start.6 = (bf16[256,23]{0,1:T(8,128)(2,1)S(1)}, bf16[256,23]{0,1:T(8,128)(2,1)}, u32[]{:S(2)}) copy-start(bf16[256,23]{0,1:T(8,128)(2,1)} %param.15) | copy-start | bytes 35332
  96.4 1.4 copy-start.3
